TPU v7x, 256 devices: a whole 4x4x8 slice. The times are simulated.
256 devices in a mesh: prow: 32 (over y, z_hi, core), pcol: 8 (over x, z_lo).
Axes of the slice: x: 4, y: 4, z: 8 (z_hi: 4, z_lo: 2; z = z_hi * 2 + z_lo), core: 2. Of those that a mesh axis runs over, the one named last changes fastest.
Arguments:
- factor_panel: float32 [2048, 63488], P('pcol', 'prow'), may hold values from -0.0234375 to 0.0234375
- whitened_before: float32 [63488, 4096], P('prow', 'pcol'), may hold values from -6 to 6
- green_panel: float32 [2048, 4096], P('prow', 'pcol'), may hold values from -6 to 6
- diag_inverse: float32 [2048, 2048], P('prow', 'pcol'), may hold values from -1 to 8, as said below
Outputs:
- whitened: float32 [2048, 4096], P('prow', 'pcol')
- gram_block: float32 [4096, 4096], P('prow', 'pcol')
Inputs may be any that keep to these rules, and one draw needn't show every extreme that they name: `diag_inverse`: zero above the diagonal and positive on it.
All inputs are finite; a program needn't handle non-finite values.
Results may differ from a plain program's by a relative error of at most 0.00012.
Values sent between devices are 32-bit elements; how exact they have to be, the bound alone decides.
A program may use at most 128 MiB of HBM per device.

v0:
```python
import jax.numpy as jnp
from jax import lax

B = 2048


def reference(factor_panel, whitened_before, green_panel, diag_inverse):
    highest = lax.Precision.HIGHEST
    remaining = green_panel - jnp.dot(
        factor_panel, whitened_before, precision=highest, preferred_element_type=jnp.float32
    )
    whitened = jnp.dot(
        diag_inverse, remaining, precision=highest, preferred_element_type=jnp.float32
    )
    gram_block = jnp.dot(
        whitened.T, whitened, precision=highest, preferred_element_type=jnp.float32
    ) * (1.0 / B)
    return (whitened, gram_block)


def solution(mesh):
    return reference
```

profile of v0, /device:TPU:36, one launch (start us, length us, event | category | flops | bytes accessed | tf_op | source)
XLA Modules:
  0.0 668.9 jit_solution(12970954545426115823)
XLA Ops:
  7.2 0.0 all-gather.12.cloned.1.call-start
  7.2 0.7 all-gather.12.cloned.1.call-update
  7.9 0.0 reduce-scatter.4.cloned.1.call-start
  7.9 322.3 %all-gather.12.cloned.1.call-done = f32[2048,1984]{0,1:T(8,128)} async-done(((f32[256,1984]{0,1:T(8,128)}), f32[2048,1984]{0,1:T(8,128)}) %all-gather.12.cloned.1.call-update) | async-done | bytes 16252944 | tf_op args[0]
  330.3 31.6 %fusion = f32[2048,512]{1,0:T(8,128)} fusion(f32[2048,1984]{0,1:T(8,128)} %all-gather.12.cloned.1.call-done, f32[1984,512]{1,0:T(8,128)} %param.2), kind=kOutput, calls=%fused_computation.2 | convolution fusion | flops 24964497408 | bytes 24510464 | tf_op jit(solution)/dot_general | solution.py:9
  361.9 0.0 copy-start.1
  361.9 0.0 copy-start.2
  361.9 0.0 reduce-scatter.4.cloned.1.call-update
  361.9 0.0 all-gather.14.cloned.1.call-start
  362.0 100.0 %reduce-scatter.4.cloned.1.call-done = f32[64,512]{1,0:T(8,128)} async-done(((f32[2048,512]{1,0:T(8,128)}), f32[64,512]{1,0:T(8,128)}) %reduce-scatter.4.cloned.1.call-update) | async-done | bytes 131088
  462.0 0.0 copy-done.1
  462.0 1.6 sub.3
  463.5 0.0 all-gather.14.cloned.1.call-update
  463.6 0.0 all-gather.16.cloned.1.call-start
  463.6 0.0 copy-done.2
  463.6 29.3 %all-gather.1 = f32[64,2048]{1,0:T(8,128)S(1)} all-gather(f32[64,256]{1,0:T(8,128)S(1)} %copy-done.2), channel_id=3, replica_groups=mesh['axis_0'=32,'axis_1'=8] {'axis_1'}, dimensions={1}, use_global_device_ids=true | all-gather | bytes 589824 | tf_op args[3]
  492.9 30.6 %all-gather.14.cloned.1.call-done = f32[2048,512]{1,0:T(8,128)} async-done(((f32[64,512]{1,0:T(8,128)}), f32[2048,512]{1,0:T(8,128)}) %all-gather.14.cloned.1.call-update) | async-done | bytes 4194320 | tf_op jit(solution)/sub | solution.py:9
  523.5 4.9 fusion.1
  528.4 0.0 copy-start
  528.4 6.7 %collective-permute-start = (f32[512,64]{0,1:T(8,128)S(1)}, f32[512,64]{0,1:T(8,128)S(1)}, u32[]{:S(2)}, u32[]{:S(2)}) collective-permute-start(f32[512,64]{0,1:T(8,128)S(1)} %fusion.1), channel_id=6, source_target_pairs={{0,0},{8,8},{16,16},{24,24},{32,1},{40,9},{48,17},{56,25},{64,2},{... | collective-permute-start | bytes 393224 | tf_op jit(solution)/dot_general | solution.py:12
  535.2 11.7 %collective-permute-done = f32[512,64]{0,1:T(8,128)S(1)} collective-permute-done((f32[512,64]{0,1:T(8,128)S(1)}, f32[512,64]{0,1:T(8,128)S(1)}, u32[]{:S(2)}, u32[]{:S(2)}) %collective-permute-start) | collective-permute-done | bytes 131104 | tf_op jit(solution)/dot_general | solution.py:12
  546.9 8.6 %all-to-all.2 = f32[4,128,64]{1,2,0:T(8,128)} all-to-all(f32[4,128,64]{1,2,0:T(8,128)S(1)} %copy_bitcast_fusion), channel_id=7, replica_groups=mesh['prow'=32,'pcol'=8] {'prow':(8)4}, dimensions={0} | all-to-all | bytes 262144 | tf_op jit(solution)/dot_general | solution.py:12
  555.4 0.0 all-gather.16.cloned.1.call-update
  555.5 0.2 all-gather.18.cloned.1.call-start
  555.7 0.0 copy-done
  555.7 0.3 all-gather.18.cloned.1.call-update
  556.1 35.8 %all-gather.16.cloned.1.call-done = f32[128,2048]{0,1:T(8,128)} async-done(((f32[128,256]{0,1:T(8,128)}), f32[128,2048]{0,1:T(8,128)}) %all-gather.16.cloned.1.call-update) | async-done | bytes 1048592 | tf_op jit(solution)/dot_general | solution.py:12
  591.9 64.6 %all-gather.18.cloned.1.call-done = f32[512,2048]{0,1:T(8,128)} async-done(((f32[512,64]{0,1:T(8,128)}), f32[512,2048]{0,1:T(8,128)}) %all-gather.18.cloned.1.call-update) | async-done | bytes 4194320 | tf_op jit(solution)/dot_general | solution.py:12
  656.5 5.8 convolution_multiply_fusion
  (1 shorter events, 0.0 us)
Async XLA Ops:
  7.2 323.1 %all-gather.12.cloned.1.call-start = ((), (), s32[]{:S(2)}) async-start(), calls=%async_computation.2 | async-start | bytes 18284544 | tf_op args[0]
  7.9 454.1 %reduce-scatter.4.cloned.1.call-start = ((), (), s32[]{:S(2)}) async-start(), calls=%async_computation.6 | async-start | bytes 4325376
  361.9 100.1 %copy-start.1 = (f32[64,512]{1,0:T(8,128)S(1)}, f32[64,512]{1,0:T(8,128)}, u32[]{:S(2)}) copy-start(f32[64,512]{1,0:T(8,128)} %param) | copy-start | bytes 393220
  361.9 101.7 %copy-start.2 = (f32[64,256]{1,0:T(8,128)S(1)}, f32[64,256]{1,0:T(8,128)}, u32[]{:S(2)}) copy-start(f32[64,256]{1,0:T(8,128)} %param.3) | copy-start | bytes 196612
  361.9 161.6 %all-gather.14.cloned.1.call-start = ((), (), s32[]{:S(2)}) async-start(), calls=%async_computation.3 | async-start | bytes 4325376 | tf_op jit(solution)/sub | solution.py:9
  463.6 128.3 %all-gather.16.cloned.1.call-start = ((), (), s32[]{:S(2)}) async-start(), calls=%async_computation.4 | async-start | bytes 1179648 | tf_op jit(solution)/dot_general | solution.py:12
  528.4 27.3 %copy-start = (f32[512,64]{0,1:T(8,128)}, f32[512,64]{0,1:T(8,128)S(1)}, u32[]{:S(2)}) copy-start(f32[512,64]{0,1:T(8,128)S(1)} %fusion.1) | copy-start | bytes 393220
  528.4 18.4 %collective-permute-start = (f32[512,64]{0,1:T(8,128)S(1)}, f32[512,64]{0,1:T(8,128)S(1)}, u32[]{:S(2)}, u32[]{:S(2)}) collective-permute-start(f32[512,64]{0,1:T(8,128)S(1)} %fusion.1), channel_id=6, source_target_pairs={{0,0},{8,8},{16,16},{24,24},{32,1},{40,9},{48,17},{56,25},{64,2},{... | collective-permute-start | bytes 393224 | tf_op jit(solution)/dot_general | solution.py:12
  555.5 101.0 %all-gather.18.cloned.1.call-start = ((), (), s32[]{:S(2)}) async-start(), calls=%async_computation.5 | async-start | bytes 4325376 | tf_op jit(solution)/dot_general | solution.py:12
Sparse Core Ops, SparseCore 0:
  9.8 320.4 all-gather.11
  362.0 99.8 reduce-scatter.3
  465.1 58.3 all-gather.13
  555.6 36.2 all-gather.15
  594.9 61.5 all-gather.17
where the time goes:
time: 672 us; the launch traced here: 669 us
  waiting for transfers between devices  566 us (84%)
  matrix products  42.4 us (6%)
  blocking collectives  37.8 us (6%)
  between operations  13.8 us (2%)
  starting transfers between devices  7.13 us (1%)
    unnamed x7, waiting for transfers between devices  423 us
    dot_general x3, waiting for transfers between devices, reference(): jnp.dot(diag_inverse, remaining, precision=highest, preferred_element_typ...  112 us
    dot_general x1, matrix products, reference(): jnp.dot(factor_panel, whitened_before, precision=highest, preferred_eleme...  31.6 us
    sub x1, waiting for transfers between devices, reference(): green_panel - jnp.dot(factor_panel, whitened_before, precision=highest, p...  30.6 us
    unnamed x1, blocking collectives  29.3 us
  transfers between devices with their start and end apart: 6, of which 6 were waited for; matrix products, arithmetic and copies ran while one was open for 0% of the time, Pallas kernels for 0%

commit v1 on v0

v1 whole, which is shorter than its diff:
```python
import jax
import jax.numpy as jnp
from jax import lax
from jax.experimental import pallas as pl
from jax.experimental.pallas import tpu as pltpu
from jax.sharding import PartitionSpec as P

F32 = jnp.float32
BF16 = jnp.bfloat16
MESH = pl.DeviceIdType.MESH
ROWS = 2048
KD = 1984
KP = 2048
NSEM = 96


def split(v):
    hi = v.astype(BF16)
    return hi, (v - hi.astype(F32)).astype(BF16)


def mm(a, b, dims):
    return lax.dot_general(a, b, (dims, ((), ())), preferred_element_type=F32)


def mm3(ah, al, bh, bl, dims):
    return mm(ah, bh, dims) + (mm(ah, bl, dims) + mm(al, bh, dims))


def kernel(ft, wb, g, di, w_out, gram_out, FT, FTh, FTl, WB, WTh, WTl, PT, RC, RY1, RY2,
           RZ1, RZ2, RG, DS, DSh, WA, LB, ssem, rsem, lsem):
    r = lax.axis_index("prow")
    c = lax.axis_index("pcol")
    core = r % 2
    z0, z1 = (r // 2) % 2, (r // 4) % 2
    y0, y1 = (r // 8) % 2, r // 16
    zl = c % 2
    x0, x1 = (c // 2) % 2, c // 4
    zh, y, x = z0 + 2 * z1, y0 + 2 * y1, x0 + 2 * x1

    def near(b0, b1, base, unit):
        p1 = base + unit * (1 - 2 * b0)
        return p1, p1 + 2 * unit * (1 - 2 * b1), base + 2 * unit * (1 - 2 * b1)

    r_core = r + 1 - 2 * core
    r_z1, r_z3, _ = near(z0, z1, r, 2)
    r_y1, r_y3, _ = near(y0, y1, r, 8)
    c_zl = c + 1 - 2 * zl
    c_x1, c_x3, _ = near(x0, x1, c, 2)
    zi1, zi3, zi2 = near(z0, z1, zh, 1)
    yi1, yi3, yi2 = near(y0, y1, y, 1)
    xi1, xi3, xi2 = near(x0, x1, x, 1)
    zlo = 1 - zl
    coreo = 1 - core
    dev = {"core": (r_core, c), "z1": (r_z1, c), "z3": (r_z3, c), "y1": (r_y1, c), "y3": (r_y3, c),
           "zl": (r, c_zl), "x1": (r, c_x1), "x3": (r, c_x3)}

    nsem = [0]
    sends = []

    def rc(src, dst, peer, rs=None, keep=True):
        i = nsem[0]
        nsem[0] += 1
        d = pltpu.make_async_remote_copy(src_ref=src, dst_ref=dst, send_sem=ssem.at[i],
                                         recv_sem=rsem.at[i if rs is None else rs],
                                         device_id=dev[peer], device_id_type=MESH)
        if keep:
            sends.append(d)
        return d

    def go(*a):
        d = rc(*a)
        d.start()
        return d

    bar = pltpu.get_barrier_semaphore()
    for p in dev.values():
        pl.semaphore_signal(bar, inc=1, device_id=p, device_id_type=MESH)
    pl.semaphore_wait(bar, len(dev))

    class Gather4:
        def __init__(self, own, slot, me, i1, i3, p1, p3):
            self.slot, self.i, self.p = slot, (me, i1, i3), (p1, p3)
            self.c1 = go(own(0), slot(me, 0), p1)
            self.c2 = go(own(1), slot(me, 1), p3)
            self.c3 = go(own(1), slot(me, 1), p1)
            self.c4 = go(own(0), slot(me, 0), p3)

        def forward(self):
            (_, i1, i3), (p1, p3) = self.i, self.p
            self.c1.wait_recv()
            self.f1 = go(self.slot(i1, 0), self.slot(i1, 0), p3)
            self.c2.wait_recv()
            self.f2 = go(self.slot(i3, 1), self.slot(i3, 1), p1)

        def near(self):
            self.c3.wait_recv()
            self.c4.wait_recv()

        def far(self):
            self.f1.wait_recv()
            self.f2.wait_recv()

    d_zl = go(di, DS.at[y, x, zl], "zl")
    wbs = []
    for q in range(4):
        cols = pl.ds(q * 128, 128)
        wbs.append((go(wb.at[:, cols], WB.at[1, q, 0:KD], "zl"),
                    go(g.at[:, cols], WB.at[1, q, KD:KP], "zl")))
    loc = []

    def lc(src, dst):
        d = pltpu.make_async_copy(src, dst, lsem.at[len(loc)])
        d.start()
        loc.append(d)

    lc(di, DS.at[y, x, zl])
    for q in range(4):
        cols = pl.ds(q * 128, 128)
        lc(wb.at[:, cols], WB.at[0, q, 0:KD])
        lc(g.at[:, cols], WB.at[0, q, KD:KP])
    lc(ft, FT.at[x])
    for d in loc:
        d.wait()

    d_zl.wait_recv()
    half_k = KD // 2
    dx = Gather4(lambda h: DS.at[y, x, h], lambda i, h: DS.at[y, i, h], x, xi1, xi3, "x1", "x3")
    dx.forward()
    dx.near()
    fx = Gather4(lambda h: FT.at[x, h * half_k:(h + 1) * half_k],
                 lambda i, h: FT.at[i, h * half_k:(h + 1) * half_k], x, xi1, xi3, "x1", "x3")
    dx.far()
    dy = Gather4(lambda h: DS.at[y, 2 * h:2 * h + 2], lambda i, h: DS.at[i, 2 * h:2 * h + 2],
                 y, yi1, yi3, "y1", "y3")

    def gray(i):
        return (i % 2 + i // 2) % 2, i // 2

    def transpose_in(h, q):
        g1, g2 = gray(q)
        pos = (2 * g1 + g2, 2 * g2 + g1)

        def step(i, _):
            k = pl.multiple_of(i * 256, 256)
            hi, lo = split(WB[h, q, pl.ds(k, 256), :].T)
            for ck in range(2):
                for ab in range(2):
                    s = ck * 64 + ab * 32
                    t = ab * 128 + pos[ab] * 32
                    WTh[ck, t:t + 32, pl.ds(k, 256)] = hi[s:s + 32]
                    WTl[ck, t:t + 32, pl.ds(k, 256)] = lo[s:s + 32]
            return 0

        lax.fori_loop(0, KP // 256, step, 0)

    def convert(i):
        def step(j, _):
            k = pl.multiple_of(j * 64, 64)
            hi, lo = split(FT[i, pl.ds(k, 64), :])
            FTh[i, pl.ds(k, 64), :] = hi
            FTl[i, pl.ds(k, 64), :] = lo
            return 0

        lax.fori_loop(0, KD // 64, step, 0)
        a = lax.broadcasted_iota(jnp.int32, (64, 256), 0)
        b = lax.broadcasted_iota(jnp.int32, (64, 256), 1)
        mine = jnp.where(jnp.logical_and(i == y, zl == z1), 1, 0)
        e = jnp.where(b == a + (2 * z0 + core) * 64, mine, 0).astype(F32)
        FTh[i, KD:KP, :] = (-e).astype(BF16)
        FTl[i, KD:KP, :] = jnp.zeros((64, 256), BF16)

    def product(h, i, m):
        cols = pl.ds(pl.multiple_of(m * 256, 256), 256)

        def step(ck, _):
            PT[h, ck, :, cols] = mm3(WTh[ck], WTl[ck], FTh[i], FTl[i], ((1,), (0,)))
            return 0

        lax.fori_loop(0, 2, step, 0)

    for q in range(4):
        transpose_in(0, q)
    convert(x)
    product(0, x, x)
    dy.forward()
    fx.forward()
    fx.near()
    for i in (xi1, xi3):
        convert(i)
        product(0, i, i)
    fx.far()
    convert(xi2)
    product(0, xi2, xi2)
    dy.near()
    dy.far()

    u1, u2 = (y0 + y1) % 2, y1
    v1, v2 = (z0 + z1) % 2, z1

    def al(v, n):
        return pl.multiple_of(v, n)

    def reduce_to_owner(h):
        own = PT.at[h, core]
        d = go(PT.at[h, coreo], RC.at[h], "core")
        d.wait_recv()

        def add_core(i, _):
            s = pl.ds(al(i * 32, 32), 32)
            PT[h, core, s, :] = PT[h, core, s, :] + RC[h, s, :]
            return 0

        lax.fori_loop(0, 8, add_core, 0)

        def exchange(offs, size, buf, first, second, keeps):
            ds_ = []
            for ab in range(2):
                src = own.at[pl.ds(al(offs[ab] + (1 - keeps[ab]) * size, size), size)]
                ds_.append(go(src, buf.at[h, ab], (first, second)[ab]))
            new = [al(offs[ab] + keeps[ab] * size, size) for ab in range(2)]
            for ab in range(2):
                ds_[ab].wait_recv()
                s = pl.ds(new[ab], size)
                PT[h, core, s, :] = PT[h, core, s, :] + buf[h, ab]
            return new

        offs = exchange([0, 128], 64, RY1, "y1", "y3", (u1, u2))
        offs = exchange(offs, 32, RY2, "y3", "y1", (u2, u1))
        offs = exchange(offs, 16, RZ1, "z1", "z3", (v1, v2))
        return exchange(offs, 8, RZ2, "z3", "z1", (v2, v1))

    offs0 = reduce_to_owner(0)
    for q in range(4):
        for d in wbs[q]:
            d.wait_recv()
        transpose_in(1, q)

    def product_all(i, _):
        product(1, i, i)
        return 0

    lax.fori_loop(0, 4, product_all, 0)

    def dsplit(q, _):
        for j in range(8):
            hi, lo = split(DS[q, j // 2, j % 2])
            lanes = pl.ds((j % 2) * 1024 + (j // 2) * 256, 256)
            DSh[0, pl.ds(al(q * 64, 64), 64), lanes] = hi
            DSh[1, pl.ds(al(q * 64, 64), 64), lanes] = lo
        return 0

    offs1 = reduce_to_owner(1)

    rows_a = core * 64 + v1 * 16 + v2 * 8
    rows_b = core * 64 + 32 + v2 * 16 + v1 * 8
    rows = [al(rows_a, 8), al(rows_b, 8)]
    xz = []
    for ab in range(2):
        xz.append(go(PT.at[1, core, pl.ds(offs1[ab], 8)], RG.at[zl, pl.ds(rows[ab], 8)], "zl"))
        RG[zl, pl.ds(rows[ab], 8), :] = PT[0, core, pl.ds(offs0[ab], 8), :]
    lax.fori_loop(0, 4, dsplit, 0)
    for d in xz:
        d.wait_recv()

    def widen(starts, size, peers):
        ds_ = []
        for ab in range(2):
            s = pl.ds(al(starts[ab], size), size)
            ds_.append(go(RG.at[:, s], RG.at[:, s], peers[ab]))
        for d in ds_:
            d.wait_recv()

    widen(rows, 8, ("z3", "z1"))
    widen([core * 64 + v1 * 16, core * 64 + 32 + v2 * 16], 16, ("z1", "z3"))
    s = pl.ds(al(core * 64, 64), 64)
    go(RG.at[:, s], RG.at[:, s], "core").wait_recv()

    acc = None
    for j in range(2):
        rh, rl = split(RG[j])
        lanes = pl.ds(j * 1024, 1024)
        t = mm3(DSh[0, :, lanes], DSh[1, :, lanes], rh, rl, ((1,), (1,)))
        acc = t if acc is None else acc + t
    WA[core, y, zh] = -acc

    wz = Gather4(lambda h: WA.at[core, y, zh, 128 * h:128 * h + 128],
                 lambda i, h: WA.at[core, y, i, 128 * h:128 * h + 128], zh, zi1, zi3, "z1", "z3")
    wz.forward()
    wz.near()
    wz.far()
    wy = Gather4(lambda h: WA.at[core, y, 2 * h:2 * h + 2], lambda i, h: WA.at[core, i, 2 * h:2 * h + 2],
                 y, yi1, yi3, "y1", "y3")
    wc = [go(WA.at[core, y], WA.at[core, y], "core")]
    wy.forward()
    wy.near()
    for i in (yi1, yi3):
        wc.append(go(WA.at[core, i], WA.at[core, i], "core"))
    wy.far()
    wc.append(go(WA.at[core, yi2], WA.at[core, yi2], "core"))

    for q in range(4):
        w_out[:, q * 128:(q + 1) * 128] = WA[core, q, zh, pl.ds(al(y * 64, 64), 64), :]
    for d in wc:
        d.wait_recv()

    y2 = 2 * z0 + core
    d1 = (x0 + x1 + y0 + y1) % 2
    d2 = (x1 + y1) % 2
    dz = (zl + z1) % 2
    base = nsem[0]
    cp = {}
    for p in ("x1", "x3", "zl"):
        for t in range(4):
            piece = LB.at[t // 2, 2 * (t % 2):2 * (t % 2) + 2]
            src = WA.at[t // 2, y2, 2 * (t % 2):2 * (t % 2) + 2]
            i = nsem[0]
            nsem[0] += 1
            for from_wa in (True, False):
                cp[p, t, from_wa] = pltpu.make_async_remote_copy(
                    src_ref=src if from_wa else piece, dst_ref=piece, send_sem=ssem.at[i],
                    recv_sem=rsem.at[base + t], device_id=dev[p], device_id_type=MESH)

    code = dz * 4 + d2 * 2 + d1

    @pl.when(code == 0)
    def _():
        for a, b, zz in ((0, 2, 0), (1, 3, 2), (2, 0, 1), (3, 1, 3)):
            cp["x1", a, True].start()
            cp["x3", b, True].start()
            cp["zl", zz, True].start()
        for t in range(2):
            for q in range(4):
                LB[t, q] = WA[t, y2, q]
        for p in ("x1", "x3", "zl"):
            for t in range(4):
                cp[p, t, True].wait_send()

    def relay(order, onward):
        for t in order:
            cp["zl", t, False].wait_recv()
            if t in onward:
                cp[onward[t], t, False].start()
            cp["zl", t, False].start()
        for t in order:
            if t in onward:
                cp[onward[t], t, False].wait_send()
            cp["zl", t, False].wait_send()

    @pl.when(code == 1)
    def _():
        relay((0, 1, 2, 3), {0: "x3", 1: "x3"})

    @pl.when(code == 2)
    def _():
        relay((2, 3, 0, 1), {2: "x1", 3: "x1"})

    @pl.when(code == 3)
    def _():
        relay((0, 2, 1, 3), {})

    @pl.when(dz == 1)
    def _():
        for t in range(4):
            cp["zl", t, False].wait_recv()

    gram_out[...] = jnp.zeros_like(gram_out)

    def gram_step(i, _):
        a, b = i // 4, i % 4
        lh, ll = split(LB[a, b].T)
        for q in range(4):
            rh, rl = split(WA[a, q, b])
            lanes = slice(q * 128, (q + 1) * 128)
            gram_out[:, lanes] = gram_out[:, lanes] + mm3(lh, ll, rh, rl, ((1,), (0,)))
        return 0

    lax.fori_loop(0, 8, gram_step, 0)
    gram_out[...] = gram_out[...] * (1.0 / ROWS)
    for d in sends:
        d.wait_send()
    assert nsem[0] <= NSEM


def body(f, wb, g, di):
    ft = f.T
    vm, dma = pltpu.VMEM, pltpu.SemaphoreType.DMA
    return pl.pallas_call(
        kernel,
        out_shape=(jax.ShapeDtypeStruct((64, 512), F32), jax.ShapeDtypeStruct((128, 512), F32)),
        in_specs=[pl.BlockSpec(memory_space=pl.ANY)] * 4,
        out_specs=(pl.BlockSpec(memory_space=pltpu.VMEM),) * 2,
        scratch_shapes=[
            vm((4, KD, 256), F32), vm((4, KP, 256), BF16), vm((4, KP, 256), BF16),
            vm((2, 4, KP, 128), F32), vm((2, 256, KP), BF16), vm((2, 256, KP), BF16),
            vm((2, 2, 256, 1024), F32), vm((2, 256, 1024), F32),
            vm((2, 2, 64, 1024), F32), vm((2, 2, 32, 1024), F32),
            vm((2, 2, 16, 1024), F32), vm((2, 2, 8, 1024), F32),
            vm((2, 128, 1024), F32), vm((4, 4, 2, 64, 256), F32), vm((2, 256, 2048), BF16),
            vm((2, 4, 4, 256, 128), F32), vm((2, 4, 256, 128), F32),
            dma((NSEM,)), dma((NSEM,)), dma((10,)),
        ],
        compiler_params=pltpu.CompilerParams(collective_id=0, has_side_effects=True,
                                             vmem_limit_bytes=66_000_000),
        name="panel",
    )(ft, wb, g, di)


def solution(mesh):
    return jax.shard_map(
        body, mesh=mesh,
        in_specs=(P("pcol", "prow"), P("prow", "pcol"), P("prow", "pcol"), P("prow", "pcol")),
        out_specs=(P("prow", "pcol"), P("prow", "pcol")), check_vma=False)
```

time: 672 us -> 246 us (0.37)
  waiting for transfers between devices: 566 us -> 0 us
  Pallas kernels: 0 us -> 242 us
  matrix products: 42.4 us -> 0 us
  blocking collectives: 37.8 us -> 0 us
  between operations: 13.8 us -> 0.64 us
  starting transfers between devices: 7.13 us -> 0 us
    unnamed x7 -> x0, waiting for transfers between devices: 423 us -> none
    pallas_call x0 -> x1, Pallas kernels: none -> 242 us  [body(): pl.pallas_call(kernel, out_shape=(jax.ShapeDtypeStruct((64, 512), F32), j...]
    dot_general x3 -> x0, waiting for transfers between devices: 112 us -> none  [reference(): jnp.dot(diag_inverse, remaining, precision=highest, preferred_element_typ...]
    dot_general x3 -> x0, matrix products: 42.4 us -> none  [the longest x1 31.6 us: reference(): jnp.dot(factor_panel, whitened_before, precision=highest, preferred_eleme...]
    sub x1 -> x0, waiting for transfers between devices: 30.6 us -> none  [reference(): green_panel - jnp.dot(factor_panel, whitened_before, precision=highest, p...]
    unnamed x1 -> x0, blocking collectives: 29.3 us -> none
    dot_general x1 -> x0, blocking collectives: 8.55 us -> none  [reference(): jnp.dot(diag_inverse, remaining, precision=highest, preferred_element_typ...]
    dot_general x3 -> x0, starting transfers between devices: 7.01 us -> none  [reference(): jnp.dot(diag_inverse, remaining, precision=highest, preferred_element_typ...]
  transfers between devices with their start and end apart: 6 -> 0, of which waited for: 6 -> 0; matrix products, arithmetic and copies ran while one was open for 0% -> 0% of each run, Pallas kernels for 0% -> 0%
where the time goes in v1:
time: 246 us
  Pallas kernels  242 us (98%)
  local copies, waits for them, and re-layouts  3.24 us (1%)
    pallas_call x1, Pallas kernels, body(): pl.pallas_call(kernel, out_shape=(jax.ShapeDtypeStruct((64, 512), F32), j...  242 us

profile of v1, /device:TPU:36, one launch (start us, length us, event | category | flops | bytes accessed | tf_op | source)
XLA Modules:
  0.0 246.2 jit_solution(8060500033866315314)
XLA Ops:
  0.6 242.4 %panel.1 = (f32[64,512]{1,0:T(8,128)}, f32[128,512]{1,0:T(8,128)}) custom-call(f32[1984,256]{1,0:T(8,128)} %bitcast.1, f32[1984,512]{1,0:T(8,128)} %wb.1, f32[64,512]{1,0:T(8,128)} %g.1, f32[64,256]{1,0:T(8,128)} %di.1), custom_call_target="tpu_custom_call" | custom-call | tf_op jit(solution)/shard_map/panel/pallas_call | solution.py:388
  243.0 1.6 copy.8
  244.6 1.7 copy.9

commit v2 on v1

v2 whole, which is shorter than its diff:
```python
import jax
import jax.numpy as jnp
from jax import lax
from jax.experimental import pallas as pl
from jax.experimental.pallas import tpu as pltpu
from jax.sharding import PartitionSpec as P

F32 = jnp.float32
BF16 = jnp.bfloat16
MESH = pl.DeviceIdType.MESH
ROWS = 2048
KD = 1984
KP = 2048
NSEM = 140
CUTS = (0, 512, 1024, 1536, 1792, KD)


def split(v):
    hi = v.astype(BF16)
    return hi, (v - hi.astype(F32)).astype(BF16)


def mm(a, b, dims):
    return lax.dot_general(a, b, (dims, ((), ())), preferred_element_type=F32)


def mm3(ah, al, bh, bl, dims):
    return mm(ah, bh, dims) + (mm(ah, bl, dims) + mm(al, bh, dims))


def kernel(ft, wb, g, di, w_out, gram_out, FT, FTh, FTl, WB, WTh, WTl, PT, RC, RYa, RYb,
           RZa, RZb, RG, DS, DSh, WA, LB, TW, ssem, rsem, lsem):
    r = lax.axis_index("prow")
    c = lax.axis_index("pcol")
    core = r % 2
    z0, z1 = (r // 2) % 2, (r // 4) % 2
    y0, y1 = (r // 8) % 2, r // 16
    zl = c % 2
    x0, x1 = (c // 2) % 2, c // 4
    zh, y, x = z0 + 2 * z1, y0 + 2 * y1, x0 + 2 * x1

    def near(b0, b1, base, unit):
        p1 = base + unit * (1 - 2 * b0)
        return p1, p1 + 2 * unit * (1 - 2 * b1), base + 2 * unit * (1 - 2 * b1)

    r_core = r + 1 - 2 * core
    r_z1, r_z3, _ = near(z0, z1, r, 2)
    r_y1, r_y3, _ = near(y0, y1, r, 8)
    c_zl = c + 1 - 2 * zl
    c_x1, c_x3, _ = near(x0, x1, c, 2)
    zi1, zi3, zi2 = near(z0, z1, zh, 1)
    yi1, yi3, yi2 = near(y0, y1, y, 1)
    xi1, xi3, xi2 = near(x0, x1, x, 1)
    zlo = 1 - zl
    coreo = 1 - core
    dev = {"core": (r_core, c), "z1": (r_z1, c), "z3": (r_z3, c), "y1": (r_y1, c), "y3": (r_y3, c),
           "zl": (r, c_zl), "x1": (r, c_x1), "x3": (r, c_x3)}

    nsem = [0]
    sends = []

    def rc(src, dst, peer, rs=None, keep=True):
        i = nsem[0]
        nsem[0] += 1
        d = pltpu.make_async_remote_copy(src_ref=src, dst_ref=dst, send_sem=ssem.at[i],
                                         recv_sem=rsem.at[i if rs is None else rs],
                                         device_id=dev[peer], device_id_type=MESH)
        if keep:
            sends.append(d)
        return d

    def go(*a):
        d = rc(*a)
        d.start()
        return d

    bar = pltpu.get_barrier_semaphore()
    for p in dev.values():
        pl.semaphore_signal(bar, inc=1, device_id=p, device_id_type=MESH)
    pl.semaphore_wait(bar, len(dev))

    class Gather4:
        def __init__(self, own, slot, me, i1, i3, p1, p3):
            self.slot, self.i, self.p = slot, (me, i1, i3), (p1, p3)
            self.c1 = go(own(0), slot(me, 0), p1)
            self.c2 = go(own(1), slot(me, 1), p3)
            self.c3 = go(own(1), slot(me, 1), p1)
            self.c4 = go(own(0), slot(me, 0), p3)

        def forward(self):
            (_, i1, i3), (p1, p3) = self.i, self.p
            self.c1.wait_recv()
            self.f1 = go(self.slot(i1, 0), self.slot(i1, 0), p3)
            self.c2.wait_recv()
            self.f2 = go(self.slot(i3, 1), self.slot(i3, 1), p1)

        def near(self):
            self.c3.wait_recv()
            self.c4.wait_recv()

        def far(self):
            self.f1.wait_recv()
            self.f2.wait_recv()

    d_zl = go(di, DS.at[y, x, zl], "zl")
    d_g = go(g, WB.at[1, KD:KP], "zl")
    wbs = [go(wb.at[a:b], WB.at[1, a:b], "zl") for a, b in zip(CUTS[:-1], CUTS[1:])]
    loc = []

    def lc(src, dst):
        d = pltpu.make_async_copy(src, dst, lsem.at[len(loc)])
        d.start()
        loc.append(d)

    lc(di, DS.at[y, x, zl])
    lc(wb, WB.at[0, 0:KD])
    lc(g, WB.at[0, KD:KP])
    lc(ft, FT.at[x])
    for d in loc:
        d.wait()

    d_zl.wait_recv()
    half_k = KD // 2
    dx = Gather4(lambda h: DS.at[y, x, h], lambda i, h: DS.at[y, i, h], x, xi1, xi3, "x1", "x3")
    dx.forward()
    dx.near()
    fx = Gather4(lambda h: FT.at[x, h * half_k:(h + 1) * half_k],
                 lambda i, h: FT.at[i, h * half_k:(h + 1) * half_k], x, xi1, xi3, "x1", "x3")
    dx.far()
    dy = Gather4(lambda h: DS.at[y, 2 * h:2 * h + 2], lambda i, h: DS.at[i, 2 * h:2 * h + 2],
                 y, yi1, yi3, "y1", "y3")

    def transpose_in(h, q, k0, k1):
        qi = 2 * ((q % 2 + q // 2) % 2) + q // 2

        def step(i, _):
            k = pl.multiple_of(i * 256, 256)
            hi, lo = split(WB[h, pl.ds(k, 256), q * 128:(q + 1) * 128].T)
            for s in range(2):
                for ck in range(2):
                    f = s * 64 + ck * 32
                    t = ck * 128 + qi * 32
                    WTh[s, t:t + 32, pl.ds(k, 256)] = hi[f:f + 32]
                    WTl[s, t:t + 32, pl.ds(k, 256)] = lo[f:f + 32]
            return 0

        lax.fori_loop(k0 // 256, k1 // 256, step, 0)

    def convert(i):
        def step(j, _):
            k = pl.multiple_of(j * 64, 64)
            hi, lo = split(FT[i, pl.ds(k, 64), :])
            FTh[i, pl.ds(k, 64), :] = hi
            FTl[i, pl.ds(k, 64), :] = lo
            return 0

        lax.fori_loop(0, KD // 64, step, 0)
        a = lax.broadcasted_iota(jnp.int32, (64, 256), 0)
        b = lax.broadcasted_iota(jnp.int32, (64, 256), 1)
        mine = jnp.where(jnp.logical_and(i == y, zl == z1), 1, 0)
        e = jnp.where(b == a + (2 * z0 + core) * 64, mine, 0).astype(F32)
        FTh[i, KD:KP, :] = (-e).astype(BF16)
        FTl[i, KD:KP, :] = jnp.zeros((64, 256), BF16)

    def product(h, i, m, k0, k1, s_all, add):
        cols = pl.ds(pl.multiple_of(m * 256, 256), 256)

        def step(s, _):
            t = mm3(WTh[s, :, k0:k1], WTl[s, :, k0:k1], FTh[i, k0:k1], FTl[i, k0:k1], ((1,), (0,)))
            t = t.reshape(2, 2, 2, 2, 2, 8, 256)
            at = (s, h) + (slice(None),) * 6 + (cols,)
            PT[at] = PT[at] + t if add else t
            return 0

        lax.fori_loop(s_all[0], s_all[-1] + 1, step, 0)

    def product_all(h, k0, k1, s_all, add):
        def one(i, _):
            product(h, i, i, k0, k1, s_all, add)
            return 0

        lax.fori_loop(0, 4, one, 0)

    both = (0, 1)
    for q in range(4):
        transpose_in(0, q, 0, KP)
    convert(x)
    product(0, x, x, 0, KP, both, False)
    dy.forward()
    fx.forward()
    fx.near()
    for i in (xi1, xi3):
        convert(i)
        product(0, i, i, 0, KP, both, False)
    fx.far()
    convert(xi2)
    product(0, xi2, xi2, 0, KP, both, False)

    u1, u2 = (y0 + y1) % 2, y1
    v1, v2 = (z0 + z1) % 2, z1

    def al(v, n):
        return pl.multiple_of(v, n)

    LA, LB_ = slice(0, 512), slice(512, 1024)
    every = slice(None)

    def reduce_to_owner(s, h):
        d = go(PT.at[s, h, coreo], RC.at[s, h], "core")
        yield
        d.wait_recv()
        for i in range(2):
            PT[s, h, core, i] = PT[s, h, core, i] + RC[s, h, i]

        def swap(buf, a_to, a_send, a_keep, b_to, b_send, b_keep):
            def part(i, lanes):
                return (s, h, core) + i + (every,) * (5 - len(i)) + (lanes,)

            da = go(PT.at[part(a_send, LA)], buf.at[s, h, 0], a_to)
            db = go(PT.at[part(b_send, LB_)], buf.at[s, h, 1], b_to)
            yield
            for d_, keep, lanes, i in ((da, a_keep, LA, 0), (db, b_keep, LB_, 1)):
                d_.wait_recv()
                at = part(keep, lanes)
                PT[at] = PT[at] + buf[s, h, i]

        def full(*idx):
            return idx

        yield from swap(RYa, "y1", full(1 - u1), full(u1), "y3", full(every, 1 - u2), full(every, u2))
        yield from swap(RYb, "y3", full(u1, 1 - u2), full(u1, u2), "y1", full(1 - u1, u2), full(u1, u2))
        yield from swap(RZa, "z1", full(u1, u2, 1 - v1), full(u1, u2, v1),
                        "z3", full(u1, u2, every, 1 - v2), full(u1, u2, every, v2))
        yield from swap(RZb, "z3", full(u1, u2, v1, 1 - v2), full(u1, u2, v1, v2),
                        "z1", full(u1, u2, 1 - v1, v2), full(u1, u2, v1, v2))

    code = ((zl + z1) % 2) * 4 + ((x1 + y1) % 2) * 2 + (x0 + x1 + y0 + y1) % 2
    y2 = 2 * z0 + core
    last = []

    def spread(s):
        base = nsem[0]
        nsem[0] += 12

        def cp(p, t, from_wa):
            at = pl.ds(2 * (t % 2), 2)
            piece = LB.at[s, t // 2, at]
            return pltpu.make_async_remote_copy(
                src_ref=WA.at[s, t // 2, y2, at] if from_wa else piece, dst_ref=piece,
                send_sem=ssem.at[base + 4 * ("x1", "x3", "zl").index(p) + t],
                recv_sem=rsem.at[base + t], device_id=dev[p], device_id_type=MESH)

        @pl.when(code == 0)
        def _():
            for a, b, zz in ((0, 2, 0), (1, 3, 2), (2, 0, 1), (3, 1, 3)):
                cp("x1", a, True).start()
                cp("x3", b, True).start()
                cp("zl", zz, True).start()
            for t in range(2):
                for q in range(4):
                    LB[s, t, q] = WA[s, t, y2, q]

        roles = {1: ((0, 1, 2, 3), {0: "x3", 1: "x3"}), 2: ((2, 3, 0, 1), {2: "x1", 3: "x1"}),
                 3: ((0, 2, 1, 3), {})}
        for n in range(4):
            yield
            for k, (order, onward) in roles.items():
                @pl.when(code == k)
                def _(order=order, onward=onward):
                    t = order[n]
                    cp("zl", t, False).wait_recv()
                    if t in onward:
                        cp(onward[t], t, False).start()
                    cp("zl", t, False).start()

            @pl.when(code >= 4)
            def _():
                cp("zl", (0, 2, 1, 3)[n], False).wait_recv()

        def finish():
            @pl.when(code == 0)
            def _():
                for p in ("x1", "x3", "zl"):
                    for t in range(4):
                        cp(p, t, True).wait_send()

            for k, (order, onward) in roles.items():
                @pl.when(code == k)
                def _(onward=onward):
                    for t in range(4):
                        if t in onward:
                            cp(onward[t], t, False).wait_send()
                        cp("zl", t, False).wait_send()

        last.append(finish)

    def stream(s):
        yield from reduce_to_owner(s, 1)
        d = go(PT.at[s, 1, core, u1, u2, v1, v2], RG.at[s, zl, core, v1, v2], "zl")
        RG[s, zl, core, v1, v2] = PT[s, 0, core, u1, u2, v1, v2]
        yield
        d.wait_recv()

        def widen(*moves):
            ds_ = [go(RG.at[(s, every, core) + i + (every, lanes)],
                      RG.at[(s, every, core) + i + (every, lanes)], p) for i, lanes, p in moves]
            yield
            for d_ in ds_:
                d_.wait_recv()

        yield from widen(((v1, v2), LA, "z3"), ((v1, v2), LB_, "z1"))
        yield from widen(((v1, every), LA, "z1"), ((every, v2), LB_, "z3"))
        d = go(RG.at[s, :, core], RG.at[s, :, core], "core")
        yield
        d.wait_recv()
        acc = None
        for j in range(2):
            rh, rl = split(RG[s, j].reshape(64, 1024))
            lanes = pl.ds(j * 1024, 1024)
            t = mm3(rh, rl, DSh[0, :, lanes], DSh[1, :, lanes], ((1,), (1,)))
            acc = t if acc is None else acc + t
        WA[s, core, y, zh] = -acc

        wz = Gather4(lambda h: WA.at[s, core, y, zh, 32 * h:32 * h + 32],
                     lambda i, h: WA.at[s, core, y, i, 32 * h:32 * h + 32], zh, zi1, zi3, "z1", "z3")
        yield
        wz.forward()
        yield
        wz.near()
        wz.far()
        wy = Gather4(lambda h: WA.at[s, core, y, 2 * h:2 * h + 2],
                     lambda i, h: WA.at[s, core, i, 2 * h:2 * h + 2], y, yi1, yi3, "y1", "y3")
        wc = [go(WA.at[s, core, y], WA.at[s, core, y], "core")]
        yield
        wy.forward()
        yield
        wy.near()
        for i in (yi1, yi3):
            wc.append(go(WA.at[s, core, i], WA.at[s, core, i], "core"))
        yield
        wy.far()
        wc.append(go(WA.at[s, core, yi2], WA.at[s, core, yi2], "core"))
        yield
        for d in wc:
            d.wait_recv()
        yield from spread(s)

    def advance(*gens):
        for i in gens:
            next(i)

    early = [reduce_to_owner(0, 0), reduce_to_owner(1, 0)]
    advance(*early)
    d_g.wait_recv()
    for i in range(3):
        wbs[i].wait_recv()
    for q in range(4):
        transpose_in(1, q, 0, 1536)
    advance(*early)
    product_all(1, 0, 1536, both, False)
    advance(*early)

    def dsplit(q, _):
        for j in range(8):
            hi, lo = split(DS[q, j // 2, j % 2])
            lanes = pl.ds((j % 2) * 1024 + (j // 2) * 256, 256)
            DSh[0, pl.ds(al(q * 64, 64), 64), lanes] = hi
            DSh[1, pl.ds(al(q * 64, 64), 64), lanes] = lo
        return 0

    dy.near()
    dy.far()
    lax.fori_loop(0, 4, dsplit, 0)
    wbs[3].wait_recv()
    for q in range(4):
        transpose_in(1, q, 1536, 1792)
    product_all(1, 1536, 1792, both, True)
    advance(*early)
    wbs[4].wait_recv()
    for q in range(4):
        transpose_in(1, q, 1792, KP)
    streams = [stream(0), stream(1)]
    for s in range(2):
        product_all(1, 1792, KP, (s,), True)
        advance(streams[s])
    pending = early + streams
    while pending:
        for i in list(pending):
            if next(i, "end") == "end":
                pending.remove(i)

    for q in range(4):
        blk = pl.ds(al(y1 * 128, 128), 128)
        TW[q] = jnp.concatenate([WA[0, core, q, zh, :, blk], WA[1, core, q, zh, :, blk]], axis=0).T
        w_out[:, q * 128:(q + 1) * 128] = TW[q, pl.ds(al(y0 * 64, 64), 64), :]

    gram_out[...] = jnp.zeros_like(gram_out)

    def gram_step(i, _):
        a, b = i // 4, i % 4
        lh, ll = split(jnp.concatenate([LB[0, a, b], LB[1, a, b]], axis=0))
        rh, rl = split(jnp.concatenate([WA[s, a, q, b] for q in range(4) for s in range(2)], axis=0))
        gram_out[...] = gram_out[...] + mm3(lh, ll, rh, rl, ((1,), (1,)))
        return 0

    lax.fori_loop(0, 8, gram_step, 0)
    gram_out[...] = gram_out[...] * (1.0 / ROWS)
    for d in sends:
        d.wait_send()
    for end in last:
        end()
    assert nsem[0] <= NSEM


def body(f, wb, g, di):
    ft = f.T
    vm, dma = pltpu.VMEM, pltpu.SemaphoreType.DMA
    return pl.pallas_call(
        kernel,
        out_shape=(jax.ShapeDtypeStruct((64, 512), F32), jax.ShapeDtypeStruct((128, 512), F32)),
        in_specs=[pl.BlockSpec(memory_space=pl.ANY)] * 4,
        out_specs=(pl.BlockSpec(memory_space=pltpu.VMEM),) * 2,
        scratch_shapes=[
            vm((4, KD, 256), F32), vm((4, KP, 256), BF16), vm((4, KP, 256), BF16),
            vm((2, KP, 512), F32), vm((2, 256, KP), BF16), vm((2, 256, KP), BF16),
            vm((2, 2, 2, 2, 2, 2, 2, 8, 1024), F32), vm((2, 2, 2, 2, 2, 2, 8, 1024), F32),
            vm((2, 2, 2, 2, 2, 2, 8, 512), F32), vm((2, 2, 2, 2, 2, 8, 512), F32),
            vm((2, 2, 2, 2, 8, 512), F32), vm((2, 2, 2, 8, 512), F32),
            vm((2, 2, 2, 2, 2, 8, 1024), F32), vm((4, 4, 2, 64, 256), F32), vm((2, 256, 2048), BF16),
            vm((2, 2, 4, 4, 64, 256), F32), vm((2, 2, 4, 64, 256), F32), vm((4, 128, 128), F32),
            dma((NSEM,)), dma((NSEM,)), dma((10,)),
        ],
        compiler_params=pltpu.CompilerParams(collective_id=0, has_side_effects=True,
                                             vmem_limit_bytes=66_000_000),
        name="panel",
    )(ft, wb, g, di)


def solution(mesh):
    return jax.shard_map(
        body, mesh=mesh,
        in_specs=(P("pcol", "prow"), P("prow", "pcol"), P("prow", "pcol"), P("prow", "pcol")),
        out_specs=(P("prow", "pcol"), P("prow", "pcol")), check_vma=False)
```

time: 246 us -> 219 us (0.89)
  Pallas kernels: 242 us -> 213 us
    pallas_call x1, Pallas kernels: 242 us -> 213 us  [body(): pl.pallas_call(kernel, out_shape=(jax.ShapeDtypeStruct((64, 512), F32), j...]
where the time goes in v2:
time: 219 us; the launch traced here: 217 us
  Pallas kernels  213 us (97%)
  local copies, waits for them, and re-layouts  3.24 us (1%)
    pallas_call x1, Pallas kernels, body(): pl.pallas_call(kernel, out_shape=(jax.ShapeDtypeStruct((64, 512), F32), j...  213 us

profile of v2, /device:TPU:36, one launch (start us, length us, event | category | flops | bytes accessed | tf_op | source)
XLA Modules:
  0.0 217.3 jit_solution(6813173911809580640)
XLA Ops:
  0.6 213.4 %panel.1 = (f32[64,512]{1,0:T(8,128)}, f32[128,512]{1,0:T(8,128)}) custom-call(f32[1984,256]{1,0:T(8,128)} %bitcast.1, f32[1984,512]{1,0:T(8,128)} %wb.1, f32[64,512]{1,0:T(8,128)} %g.1, f32[64,256]{1,0:T(8,128)} %di.1), custom_call_target="tpu_custom_call" | custom-call | tf_op jit(solution)/shard_map/panel/pallas_call | solution.py:418
  214.0 1.6 copy.8
  215.6 1.7 copy.9

commit v3 on v2

--- a/solution.py
+++ b/solution.py
@@ -12,7 +12,7 @@
 KD = 1984
 KP = 2048
 NSEM = 140
-CUTS = (0, 512, 1024, 1536, 1792, KD)
+CUTS = (0, 512, 1024, 1536, KD)
 
 
 def split(v):
@@ -28,7 +28,7 @@
     return mm(ah, bh, dims) + (mm(ah, bl, dims) + mm(al, bh, dims))
 
 
-def kernel(ft, wb, g, di, w_out, gram_out, FT, FTh, FTl, WB, WTh, WTl, PT, RC, RYa, RYb,
+def kernel(ft, wb, g, di, w_out, gram_out, FT, FTh, FTl, WB, OT, IT, WTh, WTl, PT, RC, RYa, RYb,
            RZa, RZb, RG, DS, DSh, WA, LB, TW, ssem, rsem, lsem):
     r = lax.axis_index("prow")
     c = lax.axis_index("pcol")
@@ -103,8 +103,6 @@
             self.f2.wait_recv()
 
     d_zl = go(di, DS.at[y, x, zl], "zl")
-    d_g = go(g, WB.at[1, KD:KP], "zl")
-    wbs = [go(wb.at[a:b], WB.at[1, a:b], "zl") for a, b in zip(CUTS[:-1], CUTS[1:])]
     loc = []
 
     def lc(src, dst):
@@ -112,39 +110,70 @@
         d.start()
         loc.append(d)
 
+    for a, b in zip(CUTS[:-1], CUTS[1:]):
+        lc(wb.at[a:b], WB.at[a:b])
+    lc(g, WB.at[KD:KP])
     lc(di, DS.at[y, x, zl])
-    lc(wb, WB.at[0, 0:KD])
-    lc(g, WB.at[0, KD:KP])
     lc(ft, FT.at[x])
-    for d in loc:
-        d.wait()
-
+
+    def transpose_in(k0, k1):
+        def step(i, _):
+            k = pl.multiple_of(i * 256, 256)
+            at = pl.ds(k, 256)
+            for q in range(4):
+                qi = 2 * ((q % 2 + q // 2) % 2) + q // 2
+                v = WB[at, q * 128:(q + 1) * 128].T
+                hi, lo = split(v)
+                for s in range(2):
+                    for ck in range(2):
+                        f = slice(s * 64 + ck * 32, s * 64 + ck * 32 + 32)
+                        t = slice(ck * 128 + qi * 32, ck * 128 + qi * 32 + 32)
+                        OT[s, t, at] = v[f]
+                        WTh[0, s, t, at] = hi[f]
+                        WTl[0, s, t, at] = lo[f]
+            return 0
+
+        lax.fori_loop(k0 // 256, k1 // 256, step, 0)
+
+    def swap_w(s, k0, k1):
+        return go(OT.at[s, :, k0:k1], IT.at[s, :, k0:k1], "zl")
+
+    def split_in(s, k0, k1):
+        def step(i, _):
+            at = pl.ds(pl.multiple_of(i * 32, 32), 32)
+            hi, lo = split(IT[s, at, k0:k1])
+            WTh[1, s, at, k0:k1] = hi
+            WTl[1, s, at, k0:k1] = lo
+            return 0
+
+        lax.fori_loop(0, 8, step, 0)
+
+    half_k = KD // 2
+    loc[0].wait()
+    transpose_in(0, 512)
+    loc[1].wait()
+    transpose_in(512, 1024)
+    w0 = [swap_w(0, 0, 512)]
+    loc[5].wait()
     d_zl.wait_recv()
-    half_k = KD // 2
     dx = Gather4(lambda h: DS.at[y, x, h], lambda i, h: DS.at[y, i, h], x, xi1, xi3, "x1", "x3")
+    loc[2].wait()
+    transpose_in(1024, 1536)
+    w0.append(swap_w(0, 512, 1024))
     dx.forward()
+    fx = Gather4(lambda h: ft.at[h * half_k:(h + 1) * half_k],
+                 lambda i, h: FT.at[i, h * half_k:(h + 1) * half_k], x, xi1, xi3, "x1", "x3")
+    loc[3].wait()
+    loc[4].wait()
+    transpose_in(1536, KP)
+    w0.append(swap_w(0, 1024, 1536))
+    loc[6].wait()
     dx.near()
-    fx = Gather4(lambda h: FT.at[x, h * half_k:(h + 1) * half_k],
-                 lambda i, h: FT.at[i, h * half_k:(h + 1) * half_k], x, xi1, xi3, "x1", "x3")
     dx.far()
+    w0.append(swap_w(0, 1536, KP))
     dy = Gather4(lambda h: DS.at[y, 2 * h:2 * h + 2], lambda i, h: DS.at[i, 2 * h:2 * h + 2],
                  y, yi1, yi3, "y1", "y3")
-
-    def transpose_in(h, q, k0, k1):
-        qi = 2 * ((q % 2 + q // 2) % 2) + q // 2
-
-        def step(i, _):
-            k = pl.multiple_of(i * 256, 256)
-            hi, lo = split(WB[h, pl.ds(k, 256), q * 128:(q + 1) * 128].T)
-            for s in range(2):
-                for ck in range(2):
-                    f = s * 64 + ck * 32
-                    t = ck * 128 + qi * 32
-                    WTh[s, t:t + 32, pl.ds(k, 256)] = hi[f:f + 32]
-                    WTl[s, t:t + 32, pl.ds(k, 256)] = lo[f:f + 32]
-            return 0
-
-        lax.fori_loop(k0 // 256, k1 // 256, step, 0)
+    w1 = [swap_w(1, 256 * j, 256 * j + 256) for j in range(4)]
 
     def convert(i):
         def step(j, _):
@@ -166,7 +195,7 @@
         cols = pl.ds(pl.multiple_of(m * 256, 256), 256)
 
         def step(s, _):
-            t = mm3(WTh[s, :, k0:k1], WTl[s, :, k0:k1], FTh[i, k0:k1], FTl[i, k0:k1], ((1,), (0,)))
+            t = mm3(WTh[h, s, :, k0:k1], WTl[h, s, :, k0:k1], FTh[i, k0:k1], FTl[i, k0:k1], ((1,), (0,)))
             t = t.reshape(2, 2, 2, 2, 2, 8, 256)
             at = (s, h) + (slice(None),) * 6 + (cols,)
             PT[at] = PT[at] + t if add else t
@@ -180,21 +209,6 @@
             return 0
 
         lax.fori_loop(0, 4, one, 0)
-
-    both = (0, 1)
-    for q in range(4):
-        transpose_in(0, q, 0, KP)
-    convert(x)
-    product(0, x, x, 0, KP, both, False)
-    dy.forward()
-    fx.forward()
-    fx.near()
-    for i in (xi1, xi3):
-        convert(i)
-        product(0, i, i, 0, KP, both, False)
-    fx.far()
-    convert(xi2)
-    product(0, xi2, xi2, 0, KP, both, False)
 
     u1, u2 = (y0 + y1) % 2, y1
     v1, v2 = (z0 + z1) % 2, z1
@@ -349,17 +363,6 @@
         for i in gens:
             next(i)
 
-    early = [reduce_to_owner(0, 0), reduce_to_owner(1, 0)]
-    advance(*early)
-    d_g.wait_recv()
-    for i in range(3):
-        wbs[i].wait_recv()
-    for q in range(4):
-        transpose_in(1, q, 0, 1536)
-    advance(*early)
-    product_all(1, 0, 1536, both, False)
-    advance(*early)
-
     def dsplit(q, _):
         for j in range(8):
             hi, lo = split(DS[q, j // 2, j % 2])
@@ -368,22 +371,57 @@
             DSh[1, pl.ds(al(q * 64, 64), 64), lanes] = lo
         return 0
 
+    def more():
+        k = 256 * len(w1)
+        w1.append(swap_w(1, k, k + 256))
+
+    both = (0, 1)
+    convert(x)
+    product(0, x, x, 0, KP, both, False)
+    dy.forward()
+    fx.forward()
+    fx.near()
+    more()
+    for i in (xi1, xi3):
+        convert(i)
+        product(0, i, i, 0, KP, both, False)
+    for d in w0:
+        d.wait_recv()
+    split_in(0, 0, KP)
+    for i in (x, xi1, xi3):
+        product(1, i, i, 0, KP, (0,), False)
     dy.near()
     dy.far()
     lax.fori_loop(0, 4, dsplit, 0)
-    wbs[3].wait_recv()
-    for q in range(4):
-        transpose_in(1, q, 1536, 1792)
-    product_all(1, 1536, 1792, both, True)
-    advance(*early)
-    wbs[4].wait_recv()
-    for q in range(4):
-        transpose_in(1, q, 1792, KP)
-    streams = [stream(0), stream(1)]
-    for s in range(2):
-        product_all(1, 1792, KP, (s,), True)
-        advance(streams[s])
-    pending = early + streams
+    more()
+    fx.far()
+    convert(xi2)
+    for h in range(2):
+        product(h, xi2, xi2, 0, KP, (0,), False)
+    early0, stream0 = reduce_to_owner(0, 0), stream(0)
+    advance(early0, stream0)
+    product(0, xi2, xi2, 0, KP, (1,), False)
+    early1 = reduce_to_owner(1, 0)
+    advance(early1)
+    more()
+    advance(early0, stream0)
+    for j in range(4):
+        w1[j].wait_recv()
+    split_in(1, 0, 1024)
+    product_all(1, 0, 1024, (1,), False)
+    more()
+    advance(early0, stream0, early1)
+    for j in range(4, 6):
+        w1[j].wait_recv()
+    split_in(1, 1024, 1536)
+    product_all(1, 1024, 1536, (1,), True)
+    advance(early0, stream0, early1)
+    for j in range(6, 8):
+        w1[j].wait_recv()
+        split_in(1, 256 * j, 256 * j + 256)
+        product_all(1, 256 * j, 256 * j + 256, (1,), True)
+    pending = [early0, stream0, early1, stream(1)]
+    next(pending[-1])
     while pending:
         for i in list(pending):
             if next(i, "end") == "end":
@@ -422,7 +460,8 @@
         out_specs=(pl.BlockSpec(memory_space=pltpu.VMEM),) * 2,
         scratch_shapes=[
             vm((4, KD, 256), F32), vm((4, KP, 256), BF16), vm((4, KP, 256), BF16),
-            vm((2, KP, 512), F32), vm((2, 256, KP), BF16), vm((2, 256, KP), BF16),
+            vm((KP, 512), F32), vm((2, 256, KP), F32), vm((2, 256, KP), F32),
+            vm((2, 2, 256, KP), BF16), vm((2, 2, 256, KP), BF16),
             vm((2, 2, 2, 2, 2, 2, 2, 8, 1024), F32), vm((2, 2, 2, 2, 2, 2, 8, 1024), F32),
             vm((2, 2, 2, 2, 2, 2, 8, 512), F32), vm((2, 2, 2, 2, 2, 8, 512), F32),
             vm((2, 2, 2, 2, 8, 512), F32), vm((2, 2, 2, 8, 512), F32),

time: 219 us -> 192 us (0.88)
  Pallas kernels: 213 us -> 188 us
    pallas_call x1, Pallas kernels: 213 us -> 188 us  [body(): pl.pallas_call(kernel, out_shape=(jax.ShapeDtypeStruct((64, 512), F32), j...]
where the time goes in v3:
time: 192 us
  Pallas kernels  188 us (98%)
  local copies, waits for them, and re-layouts  3.24 us (2%)
    pallas_call x1, Pallas kernels, body(): pl.pallas_call(kernel, out_shape=(jax.ShapeDtypeStruct((64, 512), F32), j...  188 us

profile of v3, /device:TPU:36, one launch (start us, length us, event | category | flops | bytes accessed | tf_op | source)
XLA Modules:
  0.0 191.5 jit_solution(12199877308731813788)
XLA Ops:
  0.6 187.7 %panel.1 = (f32[64,512]{1,0:T(8,128)}, f32[128,512]{1,0:T(8,128)}) custom-call(f32[1984,256]{1,0:T(8,128)} %bitcast.1, f32[1984,512]{1,0:T(8,128)} %wb.1, f32[64,512]{1,0:T(8,128)} %g.1, f32[64,256]{1,0:T(8,128)} %di.1), custom_call_target="tpu_custom_call" | custom-call | tf_op jit(solution)/shard_map/panel/pallas_call | solution.py:456
  188.3 1.6 copy.8
  189.9 1.7 copy.9

commit v4 on v3

--- a/solution.py
+++ b/solution.py
@@ -251,8 +251,42 @@
     code = ((zl + z1) % 2) * 4 + ((x1 + y1) % 2) * 2 + (x0 + x1 + y0 + y1) % 2
     y2 = 2 * z0 + core
     last = []
-
-    def spread(s):
+    arrived = []
+
+    def own_block(i0, i1):
+        def step(i, _):
+            a, b = i // 4, i % 4
+            at = pl.ds(al(i * 256, 256), 256)
+            for q in range(4):
+                for s in range(2):
+                    f = (q % 2) * 128 + s * 64
+                    hi, lo = split(WA[s, a, q, b])
+                    WTh[0, q // 2, f:f + 64, at] = hi
+                    WTl[0, q // 2, f:f + 64, at] = lo
+            return 0
+
+        lax.fori_loop(i0, i1, step, 0)
+
+    def gram(s):
+        lh, ll = split(jnp.concatenate([LB[s, i // 4, i % 4] for i in range(8)], axis=1))
+        for j in range(2):
+            gram_out[s * 64:s * 64 + 64, j * 256:j * 256 + 256] = mm3(
+                lh, ll, WTh[0, j], WTl[0, j], ((1,), (1,)))
+
+    def beside(n):
+        if n == 0:
+            own_block(0, 4)
+            for q in range(4):
+                blk = pl.ds(al(y1 * 128, 128), 128)
+                TW[q] = jnp.concatenate([WA[0, core, q, zh, :, blk], WA[1, core, q, zh, :, blk]], axis=0).T
+                w_out[:, q * 128:(q + 1) * 128] = TW[q, pl.ds(al(y0 * 64, 64), 64), :]
+        elif n == 1:
+            own_block(4, 8)
+        elif n == 2:
+            assert arrived
+            gram(0)
+
+    def spread(s, beside=None):
         base = nsem[0]
         nsem[0] += 12
 
@@ -291,6 +325,11 @@
             def _():
                 cp("zl", (0, 2, 1, 3)[n], False).wait_recv()
 
+            if beside is not None:
+                beside(n)
+            elif n == 3:
+                arrived.append(s)
+
         def finish():
             @pl.when(code == 0)
             def _():
@@ -333,7 +372,7 @@
             lanes = pl.ds(j * 1024, 1024)
             t = mm3(rh, rl, DSh[0, :, lanes], DSh[1, :, lanes], ((1,), (1,)))
             acc = t if acc is None else acc + t
-        WA[s, core, y, zh] = -acc
+        WA[s, core, y, zh] = acc
 
         wz = Gather4(lambda h: WA.at[s, core, y, zh, 32 * h:32 * h + 32],
                      lambda i, h: WA.at[s, core, y, i, 32 * h:32 * h + 32], zh, zi1, zi3, "z1", "z3")
@@ -357,7 +396,7 @@
         yield
         for d in wc:
             d.wait_recv()
-        yield from spread(s)
+        yield from spread(s, (None, beside)[s])
 
     def advance(*gens):
         for i in gens:
@@ -394,6 +433,7 @@
     dy.far()
     lax.fori_loop(0, 4, dsplit, 0)
     more()
+    more()
     fx.far()
     convert(xi2)
     for h in range(2):
@@ -409,7 +449,6 @@
         w1[j].wait_recv()
     split_in(1, 0, 1024)
     product_all(1, 0, 1024, (1,), False)
-    more()
     advance(early0, stream0, early1)
     for j in range(4, 6):
         w1[j].wait_recv()
@@ -427,22 +466,7 @@
             if next(i, "end") == "end":
                 pending.remove(i)
 
-    for q in range(4):
-        blk = pl.ds(al(y1 * 128, 128), 128)
-        TW[q] = jnp.concatenate([WA[0, core, q, zh, :, blk], WA[1, core, q, zh, :, blk]], axis=0).T
-        w_out[:, q * 128:(q + 1) * 128] = TW[q, pl.ds(al(y0 * 64, 64), 64), :]
-
-    gram_out[...] = jnp.zeros_like(gram_out)
-
-    def gram_step(i, _):
-        a, b = i // 4, i % 4
-        lh, ll = split(jnp.concatenate([LB[0, a, b], LB[1, a, b]], axis=0))
-        rh, rl = split(jnp.concatenate([WA[s, a, q, b] for q in range(4) for s in range(2)], axis=0))
-        gram_out[...] = gram_out[...] + mm3(lh, ll, rh, rl, ((1,), (1,)))
-        return 0
-
-    lax.fori_loop(0, 8, gram_step, 0)
-    gram_out[...] = gram_out[...] * (1.0 / ROWS)
+    gram(1)
     for d in sends:
         d.wait_send()
     for end in last:
@@ -453,7 +477,7 @@
 def body(f, wb, g, di):
     ft = f.T
     vm, dma = pltpu.VMEM, pltpu.SemaphoreType.DMA
-    return pl.pallas_call(
+    w, gram = pl.pallas_call(
         kernel,
         out_shape=(jax.ShapeDtypeStruct((64, 512), F32), jax.ShapeDtypeStruct((128, 512), F32)),
         in_specs=[pl.BlockSpec(memory_space=pl.ANY)] * 4,
@@ -473,6 +497,7 @@
                                              vmem_limit_bytes=66_000_000),
         name="panel",
     )(ft, wb, g, di)
+    return -w, gram * (1.0 / ROWS)
 
 
 def solution(mesh):

time: 192 us -> 192 us (level)
  other arithmetic: 0 us -> 3.24 us
  local copies, waits for them, and re-layouts: 3.24 us -> 0 us
    unnamed x2 -> x0, local copies, waits for them, and re-layouts: 3.24 us -> none
where the time goes in v4:
time: 192 us
  Pallas kernels  188 us (98%)
  other arithmetic  3.24 us (2%)
    pallas_call x1, Pallas kernels, body(): pl.pallas_call(kernel, out_shape=(jax.ShapeDtypeStruct((64, 512), F32), j...  188 us

profile of v4, /device:TPU:36, one launch (start us, length us, event | category | flops | bytes accessed | tf_op | source)
XLA Modules:
  0.0 192.2 jit_solution(15625402280603131984)
XLA Ops:
  0.6 188.3 %panel.1 = (f32[64,512]{1,0:T(8,128)}, f32[128,512]{1,0:T(8,128)}) custom-call(f32[1984,256]{1,0:T(8,128)} %bitcast.1, f32[1984,512]{1,0:T(8,128)} %wb.1, f32[64,512]{1,0:T(8,128)} %g.1, f32[64,256]{1,0:T(8,128)} %di.1), custom_call_target="tpu_custom_call" | custom-call | tf_op jit(solution)/shard_map/panel/pallas_call | solution.py:480
  188.9 1.6 neg.3
  190.5 1.7 broadcast_multiply_fusion

commit v5 on v4

--- a/solution.py
+++ b/solution.py
@@ -150,19 +150,21 @@
 
     half_k = KD // 2
     loc[0].wait()
-    transpose_in(0, 512)
-    loc[1].wait()
-    transpose_in(512, 1024)
-    w0 = [swap_w(0, 0, 512)]
+    transpose_in(0, 256)
+    transpose_in(256, 512)
+    w0 = [swap_w(0, 0, 256)]
     loc[5].wait()
     d_zl.wait_recv()
     dx = Gather4(lambda h: DS.at[y, x, h], lambda i, h: DS.at[y, i, h], x, xi1, xi3, "x1", "x3")
+    loc[1].wait()
+    transpose_in(512, 1024)
+    w0.append(swap_w(0, 256, 512))
+    dx.forward()
+    fx = Gather4(lambda h: ft.at[h * half_k:(h + 1) * half_k],
+                 lambda i, h: FT.at[i, h * half_k:(h + 1) * half_k], x, xi1, xi3, "x1", "x3")
     loc[2].wait()
     transpose_in(1024, 1536)
     w0.append(swap_w(0, 512, 1024))
-    dx.forward()
-    fx = Gather4(lambda h: ft.at[h * half_k:(h + 1) * half_k],
-                 lambda i, h: FT.at[i, h * half_k:(h + 1) * half_k], x, xi1, xi3, "x1", "x3")
     loc[3].wait()
     loc[4].wait()
     transpose_in(1536, KP)
@@ -321,9 +323,10 @@
                         cp(onward[t], t, False).start()
                     cp("zl", t, False).start()
 
-            @pl.when(code >= 4)
-            def _():
-                cp("zl", (0, 2, 1, 3)[n], False).wait_recv()
+            for k, order in ((4, (0, 2, 1, 3)), (5, (0, 1, 2, 3)), (6, (2, 3, 0, 1)), (7, (0, 2, 1, 3))):
+                @pl.when(code == k)
+                def _(order=order):
+                    cp("zl", order[n], False).wait_recv()
 
             if beside is not None:
                 beside(n)

time: 192 us -> 191 us (level)
  Pallas kernels: 188 us -> 186 us
    pallas_call x1, Pallas kernels: 188 us -> 186 us  [body(): pl.pallas_call(kernel, out_shape=(jax.ShapeDtypeStruct((64, 512), F32), j...]
where the time goes in v5:
time: 191 us; the launch traced here: 190 us
  Pallas kernels  186 us (97%)
  other arithmetic  3.24 us (2%)
    pallas_call x1, Pallas kernels, body(): pl.pallas_call(kernel, out_shape=(jax.ShapeDtypeStruct((64, 512), F32), j...  186 us

profile of v5, /device:TPU:36, one launch (start us, length us, event | category | flops | bytes accessed | tf_op | source)
XLA Modules:
  0.0 190.1 jit_solution(18374837268986146999)
XLA Ops:
  0.6 186.2 %panel.1 = (f32[64,512]{1,0:T(8,128)}, f32[128,512]{1,0:T(8,128)}) custom-call(f32[1984,256]{1,0:T(8,128)} %bitcast.1, f32[1984,512]{1,0:T(8,128)} %wb.1, f32[64,512]{1,0:T(8,128)} %g.1, f32[64,256]{1,0:T(8,128)} %di.1), custom_call_target="tpu_custom_call" | custom-call | tf_op jit(solution)/shard_map/panel/pallas_call | solution.py:483
  186.9 1.6 neg.3
  188.5 1.7 broadcast_multiply_fusion
